TPU v7x, 32 devices: a whole 2x2x4 slice. The times are simulated.
32 devices in a mesh: groups: 2 (over x), samp: 16 (over z, y, core).
Axes of the slice: x: 2, y: 2, z: 4, core: 2. Of those that a mesh axis runs over, the one named last changes fastest.
Arguments:
- dosage: bfloat16 [8192, 8192], P(('groups', 'samp')), parts along dimension 0, may hold values from 0 to 2
- covariates: bfloat16 [8192, 96], P(('groups', 'samp')), parts along dimension 0, may hold values from -8 to 8
- expression: bfloat16 [8192, 8192], P('groups', 'samp'), parts along dimension 0, may hold values from -10 to 10
- block_index: int32 [4, 1024], P('groups'), parts along dimension 0, may hold values from 0 to 8191
- expr_row: int32 [8192], P('groups'), parts along dimension 0, may hold values from 0 to 4095, each once
Outputs:
- zscore: float32 [4096, 8192], P('groups', 'samp'), parts along dimension 0
There are 2 independent parts, one for each index of `groups`. A program takes and returns all parts, laid end to end along the dimension named above; each array names one. Nothing has to cross between parts.
Inputs may be any that keep to these rules, and one draw needn't show every extreme that they name: `expr_row`: every expression row appears once.
All inputs are finite; a program needn't handle non-finite values.
Results may differ from a plain program's by a relative error of at most 0.0029.
Values may be sent and summed in bfloat16 or wider, within the bound.
A program may use at most 192 MiB of HBM per device.

v0:
```python
import functools
import math

import jax
import jax.numpy as jnp
from jax import lax
from jax.experimental import pallas as pl
from jax.experimental.pallas import tpu as pltpu
from jax.sharding import PartitionSpec as P

epsilon = 1e-06
MESH = pl.DeviceIdType.MESH
CHUNKS = 4
SPAN = 1024


def exchange(n, scale, p_ref, c_ref, expr_ref, row_ref, out_ref, panel, covs, matched,
             ef, mf, norm_ref, gram, right, lower, lower_scaled, sq, send_sem, recv_sem):
    depth = n // 4
    me = lax.axis_index("samp")
    z, y, core = me // 4, (me // 2) % 2, me % 2
    group = lax.axis_index("groups")
    width = p_ref.shape[0] // CHUNKS
    here = p_ref.shape[1]
    samples = expr_ref.shape[0]
    covars = c_ref.shape[0]

    def index(zz, yy, cc):
        return (zz * 2 + yy) * 2 + cc

    def target(s):
        return (group, s)

    y_peer = index(z, 1 - y, core)
    core_peer = index(z, y, 1 - core)
    z_peers = [index(lax.rem(z + j, depth), y, core) for j in range(1, depth)]
    z_from = [index(lax.rem(z + depth - j, depth), y, core) for j in range(1, depth)]

    barrier = pltpu.get_barrier_semaphore()
    for peer in [y_peer, core_peer] + z_peers:
        pl.semaphore_signal(barrier, inc=1, device_id=target(peer), device_id_type=MESH)
    pl.semaphore_wait(barrier, depth + 1)

    pieces = CHUNKS + 1

    def stripe(owner):
        return pl.ds(pl.multiple_of(owner * here, here), here)

    def dst(piece, owner):
        if piece == 0:
            return covs.at[:, stripe(owner)]
        return panel.at[pl.ds((piece - 1) * width, width), stripe(owner)]

    def own(piece):
        if piece == 0:
            return c_ref
        return p_ref.at[pl.ds((piece - 1) * width, width), :]

    started = []

    def send(piece, owner, peer, src):
        k = len(started)
        copy = pltpu.make_async_remote_copy(
            src_ref=src, dst_ref=dst(piece, owner), send_sem=send_sem.at[k],
            recv_sem=recv_sem.at[piece, owner], device_id=target(peer), device_id_type=MESH)
        copy.start()
        started.append(copy)

    def arrive(piece, owner):
        pltpu.make_async_remote_copy(
            src_ref=own(piece), dst_ref=dst(piece, owner), send_sem=send_sem.at[0],
            recv_sem=recv_sem.at[piece, owner], device_id=target(y_peer),
            device_id_type=MESH).wait_recv()

    for piece in range(pieces):
        for peer in z_peers:
            send(piece, me, peer, own(piece))
        send(piece, me, y_peer, own(piece))
        send(piece, me, core_peer, own(piece))
    covs[:, stripe(me)] = c_ref[...]
    panel[:, stripe(me)] = p_ref[...]

    step = samples // 16
    lanes = ef.shape[1]
    norm_ref[...] = jnp.zeros_like(norm_ref)

    def widen(part):
        genes = slice(part * lanes, (part + 1) * lanes)

        def body(i, _):
            rows = pl.ds(pl.multiple_of(i * step, step), step)
            x = expr_ref[rows, genes].astype(jnp.float32)
            ef[rows, :] = x
            norm_ref[:, genes] += jnp.sum(x * x, axis=0, keepdims=True)
            return 0

        lax.fori_loop(0, 16, body, 0)

    def match(part, low, high):
        genes = slice(part * lanes, (part + 1) * lanes)

        def body(i, _):
            for u in range(16):
                j = i * 16 + u
                mf[pl.ds(u, 1), :] = ef[pl.ds(row_ref[j], 1), :]
            rows = pl.ds(pl.multiple_of(i * 16, 16), 16)
            matched[rows, genes] = mf[...].astype(jnp.bfloat16)
            return 0

        lax.fori_loop(low, high, body, 0)

    def late(piece):
        for src in z_from:
            other = src + 2 - 4 * y
            arrive(piece, other)
            send(piece, other, core_peer, dst(piece, other))

    span = min(SPAN, samples)
    spans = samples // span
    columns = (((1,), (1,)), ((), ()))

    def cut(j):
        return pl.ds(pl.multiple_of(j * span, span), span)

    def eliminate():
        gram[...] = jnp.zeros_like(gram)

        def add(j, _):
            c = covs[:, cut(j)]
            gram[...] += lax.dot_general(c, c, columns, preferred_element_type=jnp.float32)
            return 0

        lax.fori_loop(0, spans, add, 0)
        row = lax.broadcasted_iota(jnp.int32, (covars, covars), 0)
        lane = lax.broadcasted_iota(jnp.int32, (covars, covars), 1)
        right[...] = (row == lane).astype(jnp.float32)
        first_lane = lax.broadcasted_iota(jnp.int32, (1, covars), 1)
        first_row = lax.broadcasted_iota(jnp.int32, (covars, 1), 0)

        def body(i, _):
            g_row, r_row = gram[pl.ds(i, 1), :], right[pl.ds(i, 1), :]
            pivot = jnp.sum(jnp.where(first_lane == i, g_row, 0.0), axis=1, keepdims=True)
            g = gram[...]
            column = jnp.sum(jnp.where(lane == i, g, 0.0), axis=1, keepdims=True)
            factor = jnp.where(first_row > i, column / pivot, 0.0)
            lower[pl.ds(i, 1), :] = r_row
            lower_scaled[pl.ds(i, 1), :] = r_row / pivot
            gram[...] = g - factor * g_row
            right[...] = right[...] - factor * r_row
            return 0

        lax.fori_loop(0, covars, body, 0)

    def scan(chunk):
        rows = pl.ds(chunk * width, width)

        def load(j, total):
            return total + lax.dot_general(
                panel[rows, cut(j)], covs[:, cut(j)], columns,
                preferred_element_type=jnp.float32)

        loads = lax.fori_loop(0, spans, load, jnp.zeros((width, covars), jnp.float32))
        solved = lax.dot_general(loads, lower[...], columns, precision=lax.Precision.HIGHEST,
                                 preferred_element_type=jnp.float32)
        coeffs = jnp.dot(solved, lower_scaled[...], precision=lax.Precision.HIGHEST,
                         preferred_element_type=jnp.float32)
        parts = jnp.concatenate(terms(coeffs), axis=1)
        sq[...] = jnp.zeros_like(sq)

        def product(j, _):
            c = covs[:, cut(j)]
            fitted = jnp.dot(parts, jnp.concatenate([c, c, c], axis=0),
                             preferred_element_type=jnp.float32)
            resid = (panel[rows, cut(j)].astype(jnp.float32) - fitted).astype(jnp.bfloat16)
            wide = resid.astype(jnp.float32)
            sq[...] += jnp.sum(wide * wide, axis=1, keepdims=True)
            part = jnp.dot(resid, matched[cut(j), :], preferred_element_type=jnp.float32)

            @pl.when(j == 0)
            def _():
                out_ref[rows, :] = part

            @pl.when(j > 0)
            def _():
                out_ref[rows, :] += part
            return 0

        lax.fori_loop(0, spans, product, 0)
        out_ref[rows, :] = (scale * out_ref[rows, :] * lax.rsqrt(sq[...] + epsilon)
                            * lax.rsqrt(norm_ref[...] + epsilon))

    def stage(piece):
        for owner_z in range(depth):
            for owner_y in range(2):
                arrive(piece, index(owner_z, owner_y, 1 - core))
        if piece == 0:
            eliminate()
        else:
            scan(piece - 1)

    groups16 = samples // 16
    halves = [groups16 * p // 3 for p in range(4)]
    rest = expr_ref.shape[1] // lanes - 1
    widen(0)
    for piece in range(pieces):
        arrive(piece, y_peer)
        send(piece, y_peer, core_peer, dst(piece, y_peer))
        for src in z_from:
            arrive(piece, src)
            send(piece, src, y_peer, dst(piece, src))
            send(piece, src, core_peer, dst(piece, src))
        if piece:
            late(piece - 1)
        if piece < 3:
            match(0, halves[piece], halves[piece + 1])
        if piece == 2:
            for part in range(1, rest + 1):
                widen(part)
                match(part, 0, groups16)
        if piece >= 2:
            stage(piece - 2)
    stage(pieces - 2)
    late(pieces - 1)
    stage(pieces - 1)
    for copy in started:
        copy.wait_send()


def terms(x):
    first = x.astype(jnp.bfloat16)
    rest = x - first.astype(jnp.float32)
    second = rest.astype(jnp.bfloat16)
    return [first, second, (rest - second.astype(jnp.float32)).astype(jnp.bfloat16)]


def local(n, dosage, covariates, expression, block_index, expr_row):
    blocks, block_width = block_index.shape
    covars = covariates.shape[1]
    samples, genes = expression.shape
    variants = blocks * block_width
    scale = math.sqrt(samples - covars - 1)

    picked = jnp.take(dosage, block_index.reshape(-1), axis=1).T
    vmem = pl.BlockSpec(memory_space=pltpu.VMEM)
    depth = n // 4
    pieces = CHUNKS + 1
    sends = pieces * (depth - 1 + 2 + 1 + 2 * (depth - 1) + depth - 1)
    lanes = genes if samples * genes * 4 <= 2**23 else 128
    square = pltpu.VMEM((covars, covars), jnp.float32)
    return pl.pallas_call(
        functools.partial(exchange, n, scale),
        out_shape=jax.ShapeDtypeStruct((variants, genes), jnp.float32),
        in_specs=[vmem, vmem, vmem, pl.BlockSpec(memory_space=pltpu.SMEM)],
        out_specs=vmem,
        scratch_shapes=[
            pltpu.VMEM((variants, samples), jnp.bfloat16),
            pltpu.VMEM((covars, samples), jnp.bfloat16),
            pltpu.VMEM((samples, genes), jnp.bfloat16),
            pltpu.VMEM((samples, lanes), jnp.float32),
            pltpu.VMEM((16, lanes), jnp.float32),
            pltpu.VMEM((1, genes), jnp.float32),
            square, square, square, square,
            pltpu.VMEM((variants // CHUNKS, 1), jnp.float32),
            pltpu.SemaphoreType.DMA((sends,)),
            pltpu.SemaphoreType.DMA((pieces, n)),
        ],
        compiler_params=pltpu.CompilerParams(
            collective_id=0, has_side_effects=True, vmem_limit_bytes=63 * 2**20),
    )(picked, covariates.T, expression, expr_row)


def solution(mesh):
    placed = (
        P(("groups", "samp"), None),
        P(("groups", "samp"), None),
        P("groups", "samp"),
        P("groups", None),
        P("groups"),
    )
    return jax.shard_map(
        functools.partial(local, mesh.shape["samp"]),
        mesh=mesh, in_specs=placed, out_specs=P("groups", "samp"), check_vma=False
    )
```

profile of v0, /device:TPU:9, one launch (start us, length us, event | category | flops | bytes accessed | tf_op | source)
XLA Modules:
  0.0 165.9 jit_solution(5065114397899473858)
XLA Ops:
  0.0 0.7 compare_and_fusion
  0.7 0.7 copy.8
  1.4 6.4 %copy.6 = bf16[256,8192]{0,1:T(8,128)(2,1)} copy(bf16[256,8192]{1,0:T(8,128)(2,1)} %param.5) | data formatting | bytes 8388608 | tf_op args[0]
  7.8 9.4 %gather_fusion = bf16[2048,256]{1,0:T(8,128)(2,1)S(1)} fusion(bf16[256,8192]{0,1:T(8,128)(2,1)} %copy.6, s32[2048]{0:T(1024)S(1)} %broadcast_clamp_fusion), kind=kCustom, calls=%fused_computation | custom fusion | bytes 2105344 | tf_op jit(solution)/shard_map/jit(_take)/gather | solution.py:243
  17.2 1.2 broadcast_select_fusion.p_ref
  18.4 142.8 %shard_map.55 = f32[2048,512]{1,0:T(8,128)} custom-call(bf16[2048,256]{1,0:T(8,128)(2,1)} %broadcast_select_fusion.p_ref, bf16[96,256]{1,0:T(8,128)(2,1)} %bitcast.11, bf16[4096,512]{1,0:T(8,128)(2,1)} %expr_ref.1, s32[4096]{0:T(1024)} %row_ref.1), custom_call_target="tpu_custom_call" | custom-call | tf_op jit(solution)/shard_map/pallas_call | solution.py:250
  161.2 4.6 %copy.13 = f32[2048,512]{1,0:T(8,128)} copy(f32[2048,512]{1,0:T(8,128)} %shard_map.55) | data formatting | bytes 8388608
  (2 shorter events, 0.0 us)
where the time goes:
time: 166 us
  Pallas kernels  143 us (86%)
  local copies, waits for them, and re-layouts  21.1 us (13%)
  other arithmetic  1.95 us (1%)
    pallas_call x1, Pallas kernels, local(): pl.pallas_call(functools.partial(exchange, n, scale), out_shape=jax.Shape...  143 us
    unnamed x3, local copies, waits for them, and re-layouts  11.7 us
    gather x1, local copies, waits for them, and re-layouts, local(): picked = jnp.take(dosage, block_index.reshape(-1), axis=1).T  9.36 us

commit v1 on v0

v1 whole, which is shorter than its diff:
```python
import functools
import math

import jax
import jax.numpy as jnp
from jax import lax
from jax.experimental import pallas as pl
from jax.experimental.pallas import tpu as pltpu
from jax.sharding import PartitionSpec as P

epsilon = 1e-06
MESH = pl.DeviceIdType.MESH
CHUNKS = 8
SPAN = 1024
COLUMNS = (((1,), (1,)), ((), ()))


def terms(x):
    first = x.astype(jnp.bfloat16)
    rest = x - first.astype(jnp.float32)
    second = rest.astype(jnp.bfloat16)
    return [first, second, (rest - second.astype(jnp.float32)).astype(jnp.bfloat16)]


def exchange(n, scale, dosage, c_ref, expr, index_ref, row_ref, out_ref,
             panel, covs, mine, theirs, picked, turned, raw, lines, rows_f32, ebuf,
             norm, norm_other, part, gram, right, lower, lower_scaled, parts, sq,
             result, load_sem, expr_sem, send_sem, recv_sem, core_sem):
    depth = n // 4
    me = lax.axis_index("samp")
    z, y, core = me // 4, (me // 2) % 2, me % 2
    group = lax.axis_index("groups")
    here = picked.shape[1]
    variants = picked.shape[0]
    half = panel.shape[0]
    samples = panel.shape[1]
    genes = mine.shape[1]
    covars = covs.shape[0]
    block_width = index_ref.shape[1]
    width = half // CHUNKS
    pieces = CHUNKS + 1
    pair = 2 * here
    top, bottom = depth - 1, 0
    balance = depth >= 4

    def device(zz, yy, cc):
        return (group, (zz * 2 + yy) * 2 + cc)

    partner = device(z, y, 1 - core)
    below, above = z > bottom, z < top

    panel_width = dosage.shape[1]
    quarters = raw.shape[0]
    quarter = panel_width // quarters

    def loading(q):
        return pltpu.make_async_copy(
            dosage.at[:, pl.ds(q * quarter, quarter)], raw.at[q], load_sem.at[q])

    for q in range(quarters):
        loading(q).start()

    barrier = pltpu.get_barrier_semaphore()
    pl.semaphore_signal(barrier, inc=1, device_id=partner, device_id_type=MESH)
    for h in range(2):
        pl.semaphore_signal(barrier, inc=1, device_id=device(z, 1 - y, h), device_id_type=MESH)

        @pl.when(below)
        def _():
            pl.semaphore_signal(barrier, inc=1, device_id=device(z - 1, y, h), device_id_type=MESH)

        @pl.when(above)
        def _():
            pl.semaphore_signal(barrier, inc=1, device_id=device(z + 1, y, h), device_id_type=MESH)

    def chip(zz, yy):
        return zz * 2 + yy

    def stripe(c):
        return pl.ds(pl.multiple_of(c * pair, pair), pair)

    def single(zz, yy, cc):
        return pl.ds(pl.multiple_of(((zz * 2 + yy) * 2 + cc) * here, here), here)

    def row_range(piece):
        return pl.ds((piece - 1) * width, width)

    def block(piece, where):
        if piece == 0:
            return covs.at[:, where]
        return panel.at[row_range(piece), where]

    def own(piece, h):
        if piece == 0:
            return c_ref
        start = h * half + (piece - 1) * width
        if not isinstance(h, int):
            start = pl.multiple_of(start, width)
        return picked.at[pl.ds(start, width), :]

    started = []

    def send(when, src, dst, target, recv):
        copy = pltpu.make_async_remote_copy(
            src_ref=src, dst_ref=dst, send_sem=send_sem.at[len(started)], recv_sem=recv,
            device_id=target, device_id_type=MESH)
        if when is None:
            copy.start()
        else:
            pl.when(when)(copy.start)
        started.append((when, copy))

    def send_own(piece):
        where = single(z, y, core)
        sem = recv_sem.at[piece, chip(z, y)]
        for h in range(2):
            src = own(piece, h)
            dst = block(piece, where)
            send(None, src, dst, device(z, 1 - y, h), sem)
            send(below, src, dst, device(z - 1, y, h), sem)
            send(above, src, dst, device(z + 1, y, h), sem)
        send(None, own(piece, 1 - core), block(piece, where), partner, sem)
        if piece == 0:
            covs[:, where] = c_ref[...]
        else:
            start = pl.multiple_of(core * half + (piece - 1) * width, width)
            panel[row_range(piece), where] = picked[pl.ds(start, width), :]

    def arrive(piece, zz, yy):
        where = stripe(chip(zz, yy))
        pltpu.make_async_remote_copy(
            src_ref=block(piece, where), dst_ref=block(piece, where), send_sem=send_sem.at[0],
            recv_sem=recv_sem.at[piece, chip(zz, yy)], device_id=partner,
            device_id_type=MESH).wait_recv()

    def arrive_partner(piece):
        where = single(z, y, 1 - core)
        pltpu.make_async_remote_copy(
            src_ref=block(piece, where), dst_ref=block(piece, where), send_sem=send_sem.at[0],
            recv_sem=recv_sem.at[piece, chip(z, y)], device_id=partner,
            device_id_type=MESH).wait_recv()

    def forward(when, piece, zz, yy, target):
        where = block(piece, stripe(chip(zz, yy)))
        send(when, where, where, target, recv_sem.at[piece, chip(zz, yy)])

    down = device(z - 1, y, core)
    up = device(z + 1, y, core)
    across = device(z, 1 - y, core)

    def relay_cross(piece):
        arrive(piece, z, 1 - y)
        if balance:
            low, high = z == bottom, z == top
            if piece % 2:
                low_too, high_too = z == top - 1, z == bottom + 1
                forward(low | low_too, piece, z, 1 - y, up)
                forward(high | high_too, piece, z, 1 - y, down)
            else:
                forward(low, piece, z, 1 - y, up)
                forward(high, piece, z, 1 - y, down)

    def relay(piece, d):
        for sign in (1, -1):
            src = z + sign * d
            valid = (src <= top) if sign > 0 else (src >= bottom)
            onward = below if sign > 0 else above
            target = down if sign > 0 else up

            @pl.when(valid)
            def _():
                arrive(piece, src, y)

            forward(valid & onward, piece, src, y, target)
            cross = valid
            if balance and d == 1:
                end = (z == top - 1) if sign > 0 else (z == bottom + 1)
                cross = cross & jnp.logical_not(end)
                if piece % 2:
                    edge = (z == bottom) if sign > 0 else (z == top)
                    cross = cross & jnp.logical_not(edge)
            forward(cross, piece, src, y, across)

    def settle(piece):
        arrive_partner(piece)
        for d in range(1, depth):
            for sign in (1, -1):
                src = z + sign * d

                @pl.when((src <= top) if sign > 0 else (src >= bottom))
                def _():
                    arrive(piece, src, 1 - y)

    block_lanes = 512

    def turn(q):
        def body(i, _):
            lanes = pl.ds(pl.multiple_of(i * block_lanes, block_lanes), block_lanes)
            x = raw[q, :, lanes].astype(jnp.float32)
            rows = pl.ds(pl.multiple_of(q * quarter + i * block_lanes, block_lanes), block_lanes)
            turned[rows, :] = x.T
            return 0

        lax.fori_loop(0, quarter // block_lanes, body, 0)

    batch = lines.shape[0]

    def pick(piece):
        for h in range(2):
            first = h * half + (piece - 1) * width

            def body(i, _):
                base = first + i * batch
                b, at = base // block_width, lax.rem(base, block_width)
                for u in range(batch):
                    lines[pl.ds(u, 1), :] = turned[pl.ds(index_ref[b, at + u], 1), :]
                picked[pl.ds(pl.multiple_of(base, batch), batch), :] = (
                    lines[...].astype(jnp.bfloat16))
                return 0

            lax.fori_loop(0, width // batch, body, 0)

    lanes = here
    expr_parts = genes // lanes

    def loading_expr(p):
        return pltpu.make_async_copy(expr.at[:, pl.ds(p * lanes, lanes)], ebuf, expr_sem)

    def widen(p):
        loading_expr(p).wait()
        columns = slice(p * lanes, (p + 1) * lanes)
        step = samples // 16

        def body(i, total):
            rows = pl.ds(pl.multiple_of(i * step, step), step)
            x = ebuf[rows, :].astype(jnp.float32)
            turned[rows, :] = x
            return total + jnp.sum(x * x, axis=0, keepdims=True)

        total = lax.fori_loop(0, 16, body, jnp.zeros((1, lanes), jnp.float32))
        norm[:, columns] = jnp.broadcast_to(total, (8, lanes))
        if p + 1 < expr_parts:
            loading_expr(p + 1).start()
        else:
            send(None, norm, norm_other, partner, core_sem.at[0])

    match_parts = 4

    def match(p, q):
        columns = slice(p * lanes, (p + 1) * lanes)
        span = samples // match_parts

        def body(i, _):
            base = q * span + i * batch
            for u in range(batch):
                lines[pl.ds(u, 1), :] = turned[pl.ds(row_ref[base + u], 1), :]
            mine[pl.ds(pl.multiple_of(base, batch), batch), columns] = (
                lines[...].astype(jnp.bfloat16))
            return 0

        lax.fori_loop(0, span // batch, body, 0)

    def send_match(p, q):
        span = samples // match_parts
        where = (pl.ds(q * span, span), pl.ds(p * lanes, lanes))
        send(None, mine.at[where], theirs.at[where], partner,
             core_sem.at[1 + p * match_parts + q])

    def arrive_match():
        pltpu.make_async_remote_copy(
            src_ref=norm, dst_ref=norm_other, send_sem=send_sem.at[0],
            recv_sem=core_sem.at[0], device_id=partner, device_id_type=MESH).wait_recv()
        span = samples // match_parts
        for p in range(expr_parts):
            for q in range(match_parts):
                where = (pl.ds(q * span, span), pl.ds(p * lanes, lanes))
                pltpu.make_async_remote_copy(
                    src_ref=mine.at[where], dst_ref=theirs.at[where], send_sem=send_sem.at[0],
                    recv_sem=core_sem.at[1 + p * match_parts + q], device_id=partner,
                    device_id_type=MESH).wait_recv()

    span = min(SPAN, samples)
    spans = samples // span

    def cut(j):
        return pl.ds(pl.multiple_of(j * span, span), span)

    def make_gram():
        settle(0)
        gram[...] = jnp.zeros_like(gram)

        def add(j, _):
            c = covs[:, cut(j)]
            gram[...] += lax.dot_general(c, c, COLUMNS, preferred_element_type=jnp.float32)
            return 0

        lax.fori_loop(0, spans, add, 0)
        row = lax.broadcasted_iota(jnp.int32, (covars, covars), 0)
        lane = lax.broadcasted_iota(jnp.int32, (covars, covars), 1)
        right[...] = (row == lane).astype(jnp.float32)

    def eliminate(low, high):
        lane = lax.broadcasted_iota(jnp.int32, (covars, covars), 1)
        first_lane = lax.broadcasted_iota(jnp.int32, (1, covars), 1)
        first_row = lax.broadcasted_iota(jnp.int32, (covars, 1), 0)

        def body(i, _):
            g_row, r_row = gram[pl.ds(i, 1), :], right[pl.ds(i, 1), :]
            pivot = jnp.sum(jnp.where(first_lane == i, g_row, 0.0), axis=1, keepdims=True)
            g = gram[...]
            column = jnp.sum(jnp.where(lane == i, g, 0.0), axis=1, keepdims=True)
            factor = jnp.where(first_row > i, column / pivot, 0.0)
            lower[pl.ds(i, 1), :] = r_row
            lower_scaled[pl.ds(i, 1), :] = r_row / pivot
            gram[...] = g - factor * g_row
            right[...] = right[...] - factor * r_row
            return 0

        lax.fori_loop(low, high, body, 0)

    def solve(piece):
        settle(piece)
        rows = row_range(piece)

        def load(j, total):
            return total + lax.dot_general(
                panel[rows, cut(j)], covs[:, cut(j)], COLUMNS,
                preferred_element_type=jnp.float32)

        loads = lax.fori_loop(0, spans, load, jnp.zeros((width, covars), jnp.float32))
        solved = lax.dot_general(loads, lower[...], COLUMNS, precision=lax.Precision.HIGHEST,
                                 preferred_element_type=jnp.float32)
        coeffs = jnp.dot(solved, lower_scaled[...], precision=lax.Precision.HIGHEST,
                         preferred_element_type=jnp.float32)
        parts[...] = jnp.concatenate(terms(coeffs), axis=1)
        sq[...] = jnp.zeros_like(sq)

    def product(piece, j):
        rows = row_range(piece)
        c = covs[:, cut(j)]
        fitted = jnp.dot(parts[...], jnp.concatenate([c, c, c], axis=0),
                         preferred_element_type=jnp.float32)
        resid = (panel[rows, cut(j)].astype(jnp.float32) - fitted).astype(jnp.bfloat16)
        wide = resid.astype(jnp.float32)
        sq[...] += jnp.sum(wide * wide, axis=1, keepdims=True)
        kept = jnp.dot(resid, mine[cut(j), :], preferred_element_type=jnp.float32)
        given = jnp.dot(resid, theirs[cut(j), :], preferred_element_type=jnp.float32)
        if j == 0:
            result[rows, :] = kept
            part[rows, :] = given
        else:
            result[rows, :] += kept
            part[rows, :] += given

    def out_rows(piece):
        return pl.ds(pl.multiple_of(core * half + (piece - 1) * width, width), width)

    def finish(piece):
        rows = row_range(piece)
        size = scale * lax.rsqrt(sq[...] + epsilon)
        part[rows, :] = part[rows, :] * size * lax.rsqrt(norm_other[:1, :] + epsilon)
        out_ref[out_rows(piece), :] = result[rows, :] * size * lax.rsqrt(norm[:1, :] + epsilon)

    def give(piece):
        send(None, part.at[row_range(piece), :], out_ref.at[out_rows(piece), :], partner,
             core_sem.at[1 + expr_parts * match_parts + piece - 1])

    def receive(piece):
        rows = pl.ds(pl.multiple_of((1 - core) * half + (piece - 1) * width, width), width)
        pltpu.make_async_remote_copy(
            src_ref=part.at[row_range(piece), :], dst_ref=out_ref.at[rows, :],
            send_sem=send_sem.at[0],
            recv_sem=core_sem.at[1 + expr_parts * match_parts + piece - 1], device_id=partner,
            device_id_type=MESH).wait_recv()

    work = []

    def todo(earliest, weight, call, *args):
        work.append((earliest, weight, functools.partial(call, *args)))

    for piece in range(3, pieces):
        todo(0, 0.6, pick, piece)
    sent = None
    for p in range(expr_parts):
        todo(0, 1.0, widen, p)
        for q in range(match_parts):
            todo(0, 1.3, match, p, q)
            if sent is not None:
                todo(0, 0.0, send_match, *sent)
            sent = (p, q)
    todo(0, 0.0, send_match, *sent)
    todo(1, 0.7, make_gram)
    step = covars // 12
    for i in range(12):
        todo(1, 1.2, eliminate, i * step, covars if i == 11 else (i + 1) * step)
    todo(1, 0.0, arrive_match)
    for piece in range(1, pieces):
        todo(piece + 1, 0.6, solve, piece)
        for j in range(spans):
            todo(piece + 1, 0.5, product, piece, j)
        todo(piece + 1, 0.3, finish, piece)
        todo(piece + 1, 0.0, give, piece)

    pl.semaphore_wait(barrier, 3 + 2 * below.astype(jnp.int32) + 2 * above.astype(jnp.int32))
    send_own(0)
    for q in range(quarters):
        loading(q).wait()
        turn(q)
    loading_expr(0).start()
    pick(1)
    pick(2)
    send_own(1)
    slots = depth

    for piece in range(pieces):
        if 0 < piece and piece + 1 < pieces:
            send_own(piece + 1)
        left = sum(w for e, w, _ in work if e <= pieces - 1)
        quota = left / (pieces - piece) / slots

        def run():
            spent = 0.0
            while work and work[0][0] <= piece and (spent < quota or work[0][1] == 0.0):
                spent += work[0][1]
                work.pop(0)[2]()

        relay_cross(piece)
        run()
        for d in range(1, depth):
            relay(piece, d)
            run()
    for _, _, call in work:
        call()
    for piece in range(1, pieces):
        receive(piece)
    for when, copy in started:
        if when is None:
            copy.wait_send()
        else:
            pl.when(when)(copy.wait_send)


def local(n, dosage, covariates, expression, block_index, expr_row):
    blocks, block_width = block_index.shape
    here, covars = covariates.shape
    samples, genes = expression.shape
    variants = blocks * block_width
    half = variants // 2
    width = half // CHUNKS
    scale = math.sqrt(samples - covars - 1)
    vmem = pl.BlockSpec(memory_space=pltpu.VMEM)
    smem = pl.BlockSpec(memory_space=pltpu.SMEM)
    hbm = pl.BlockSpec(memory_space=pl.ANY)
    depth = n // 4
    pieces = CHUNKS + 1
    sends = pieces * (7 + 2 + 4 * (depth - 1)) + 64
    square = pltpu.VMEM((covars, covars), jnp.float32)
    quarters = 4
    return pl.pallas_call(
        functools.partial(exchange, n, scale),
        out_shape=jax.ShapeDtypeStruct((variants, genes), jnp.float32),
        in_specs=[hbm, vmem, hbm, smem, smem],
        out_specs=vmem,
        scratch_shapes=[
            pltpu.VMEM((half, samples), jnp.bfloat16),
            pltpu.VMEM((covars, samples), jnp.bfloat16),
            pltpu.VMEM((samples, genes), jnp.bfloat16),
            pltpu.VMEM((samples, genes), jnp.bfloat16),
            pltpu.VMEM((variants, here), jnp.bfloat16),
            pltpu.VMEM((max(dosage.shape[1], samples), here), jnp.float32),
            pltpu.VMEM((quarters, here, dosage.shape[1] // quarters), jnp.bfloat16),
            pltpu.VMEM((64, here), jnp.float32),
            pltpu.VMEM((8, 128), jnp.float32),
            pltpu.VMEM((samples, here), jnp.bfloat16),
            pltpu.VMEM((8, genes), jnp.float32),
            pltpu.VMEM((8, genes), jnp.float32),
            pltpu.VMEM((half, genes), jnp.float32),
            square, square, square, square,
            pltpu.VMEM((width, 3 * covars), jnp.bfloat16),
            pltpu.VMEM((width, 1), jnp.float32),
            pltpu.VMEM((half, genes), jnp.float32),
            pltpu.SemaphoreType.DMA((quarters,)),
            pltpu.SemaphoreType.DMA,
            pltpu.SemaphoreType.DMA((sends,)),
            pltpu.SemaphoreType.DMA((pieces, n // 2)),
            pltpu.SemaphoreType.DMA((64,)),
        ],
        compiler_params=pltpu.CompilerParams(
            collective_id=0, has_side_effects=True, vmem_limit_bytes=63 * 2**20),
    )(dosage, covariates.T, expression, block_index, expr_row)


def solution(mesh):
    placed = (
        P(("groups", "samp"), None),
        P(("groups", "samp"), None),
        P("groups", "samp"),
        P("groups", None),
        P("groups"),
    )
    return jax.shard_map(
        functools.partial(local, mesh.shape["samp"]),
        mesh=mesh, in_specs=placed, out_specs=P("groups", "samp"), check_vma=False
    )
```

time: 166 us -> 127 us (0.77)
  the two profiles are of different devices: /device:TPU:9 before, /device:TPU:1 now
where the time goes in v1:
time: 127 us
  Pallas kernels  122 us (96%)
  local copies, waits for them, and re-layouts  4.64 us (4%)
    pallas_call x1, Pallas kernels, local(): pl.pallas_call(functools.partial(exchange, n, scale), out_shape=jax.Shape...  122 us
    unnamed x1, local copies, waits for them, and re-layouts  4.64 us

profile of v1, /device:TPU:1, one launch (start us, length us, event | category | flops | bytes accessed | tf_op | source)
XLA Modules:
  0.0 126.9 jit_solution(16035438319464947178)
XLA Ops:
  0.0 122.2 %shard_map.55 = f32[2048,512]{1,0:T(8,128)} custom-call(bf16[256,8192]{1,0:T(8,128)(2,1)} %dosage.1, bf16[96,256]{1,0:T(8,128)(2,1)} %bitcast.1, bf16[4096,512]{1,0:T(8,128)(2,1)} %expr.1, s32[2,1024]{1,0:T(2,128)} %index_ref.1, s32[4096]{0:T(1024)} %row_ref.1), custom_call_target="tpu_custom_call" | custom-call | tf_op jit(solution)/shard_map/pallas_call | solution.py:459
  122.2 4.6 %copy.7 = f32[2048,512]{1,0:T(8,128)} copy(f32[2048,512]{1,0:T(8,128)} %shard_map.55) | data formatting | bytes 8388608

commit v2 on v1

--- a/solution.py
+++ b/solution.py
@@ -10,7 +10,7 @@
 
 epsilon = 1e-06
 MESH = pl.DeviceIdType.MESH
-CHUNKS = 8
+PATTERN = (1, 1, 1, 1, 1, 1, 1, 1)
 SPAN = 1024
 COLUMNS = (((1,), (1,)), ((), ()))
 
@@ -37,8 +37,9 @@
     genes = mine.shape[1]
     covars = covs.shape[0]
     block_width = index_ref.shape[1]
-    width = half // CHUNKS
-    pieces = CHUNKS + 1
+    widths = [p * half // sum(PATTERN) for p in PATTERN]
+    starts = [sum(widths[:k]) for k in range(len(widths))]
+    pieces = len(widths) + 1
     pair = 2 * here
     top, bottom = depth - 1, 0
     balance = depth >= 4
@@ -83,7 +84,7 @@
         return pl.ds(pl.multiple_of(((zz * 2 + yy) * 2 + cc) * here, here), here)
 
     def row_range(piece):
-        return pl.ds((piece - 1) * width, width)
+        return pl.ds(starts[piece - 1], widths[piece - 1])
 
     def block(piece, where):
         if piece == 0:
@@ -93,10 +94,10 @@
     def own(piece, h):
         if piece == 0:
             return c_ref
-        start = h * half + (piece - 1) * width
+        start = h * half + starts[piece - 1]
         if not isinstance(h, int):
-            start = pl.multiple_of(start, width)
-        return picked.at[pl.ds(start, width), :]
+            start = pl.multiple_of(start, 16)
+        return picked.at[pl.ds(start, widths[piece - 1]), :]
 
     started = []
 
@@ -123,8 +124,8 @@
         if piece == 0:
             covs[:, where] = c_ref[...]
         else:
-            start = pl.multiple_of(core * half + (piece - 1) * width, width)
-            panel[row_range(piece), where] = picked[pl.ds(start, width), :]
+            start = pl.multiple_of(core * half + starts[piece - 1], 16)
+            panel[row_range(piece), where] = picked[pl.ds(start, widths[piece - 1]), :]
 
     def arrive(piece, zz, yy):
         where = stripe(chip(zz, yy))
@@ -207,18 +208,19 @@
 
     def pick(piece):
         for h in range(2):
-            first = h * half + (piece - 1) * width
+            first = h * half + starts[piece - 1]
+            few = math.gcd(batch, widths[piece - 1])
 
             def body(i, _):
-                base = first + i * batch
+                base = first + i * few
                 b, at = base // block_width, lax.rem(base, block_width)
-                for u in range(batch):
+                for u in range(few):
                     lines[pl.ds(u, 1), :] = turned[pl.ds(index_ref[b, at + u], 1), :]
-                picked[pl.ds(pl.multiple_of(base, batch), batch), :] = (
-                    lines[...].astype(jnp.bfloat16))
+                picked[pl.ds(pl.multiple_of(base, few), few), :] = (
+                    lines[:few, :].astype(jnp.bfloat16))
                 return 0
 
-            lax.fori_loop(0, width // batch, body, 0)
+            lax.fori_loop(0, widths[piece - 1] // few, body, 0)
 
     lanes = here
     expr_parts = genes // lanes
@@ -327,22 +329,23 @@
                 panel[rows, cut(j)], covs[:, cut(j)], COLUMNS,
                 preferred_element_type=jnp.float32)
 
-        loads = lax.fori_loop(0, spans, load, jnp.zeros((width, covars), jnp.float32))
+        loads = lax.fori_loop(0, spans, load, jnp.zeros((widths[piece - 1], covars), jnp.float32))
         solved = lax.dot_general(loads, lower[...], COLUMNS, precision=lax.Precision.HIGHEST,
                                  preferred_element_type=jnp.float32)
         coeffs = jnp.dot(solved, lower_scaled[...], precision=lax.Precision.HIGHEST,
                          preferred_element_type=jnp.float32)
-        parts[...] = jnp.concatenate(terms(coeffs), axis=1)
+        parts[:widths[piece - 1], :] = jnp.concatenate(terms(coeffs), axis=1)
         sq[...] = jnp.zeros_like(sq)
 
     def product(piece, j):
         rows = row_range(piece)
         c = covs[:, cut(j)]
-        fitted = jnp.dot(parts[...], jnp.concatenate([c, c, c], axis=0),
+        tall = widths[piece - 1]
+        fitted = jnp.dot(parts[:tall, :], jnp.concatenate([c, c, c], axis=0),
                          preferred_element_type=jnp.float32)
         resid = (panel[rows, cut(j)].astype(jnp.float32) - fitted).astype(jnp.bfloat16)
         wide = resid.astype(jnp.float32)
-        sq[...] += jnp.sum(wide * wide, axis=1, keepdims=True)
+        sq[:tall, :] += jnp.sum(wide * wide, axis=1, keepdims=True)
         kept = jnp.dot(resid, mine[cut(j), :], preferred_element_type=jnp.float32)
         given = jnp.dot(resid, theirs[cut(j), :], preferred_element_type=jnp.float32)
         if j == 0:
@@ -353,11 +356,11 @@
             part[rows, :] += given
 
     def out_rows(piece):
-        return pl.ds(pl.multiple_of(core * half + (piece - 1) * width, width), width)
+        return pl.ds(pl.multiple_of(core * half + starts[piece - 1], 16), widths[piece - 1])
 
     def finish(piece):
         rows = row_range(piece)
-        size = scale * lax.rsqrt(sq[...] + epsilon)
+        size = scale * lax.rsqrt(sq[:widths[piece - 1], :] + epsilon)
         part[rows, :] = part[rows, :] * size * lax.rsqrt(norm_other[:1, :] + epsilon)
         out_ref[out_rows(piece), :] = result[rows, :] * size * lax.rsqrt(norm[:1, :] + epsilon)
 
@@ -366,7 +369,7 @@
              core_sem.at[1 + expr_parts * match_parts + piece - 1])
 
     def receive(piece):
-        rows = pl.ds(pl.multiple_of((1 - core) * half + (piece - 1) * width, width), width)
+        rows = pl.ds(pl.multiple_of((1 - core) * half + starts[piece - 1], 16), widths[piece - 1])
         pltpu.make_async_remote_copy(
             src_ref=part.at[row_range(piece), :], dst_ref=out_ref.at[rows, :],
             send_sem=send_sem.at[0],
@@ -389,17 +392,19 @@
                 todo(0, 0.0, send_match, *sent)
             sent = (p, q)
     todo(0, 0.0, send_match, *sent)
-    todo(1, 0.7, make_gram)
-    step = covars // 12
+    todo(depth - 1, 0.7, make_gram)
+    rounds = covars // 12
     for i in range(12):
-        todo(1, 1.2, eliminate, i * step, covars if i == 11 else (i + 1) * step)
+        todo(depth - 1, 1.2, eliminate, i * rounds,
+             covars if i == 11 else (i + 1) * rounds)
     todo(1, 0.0, arrive_match)
     for piece in range(1, pieces):
-        todo(piece + 1, 0.6, solve, piece)
+        share = widths[piece - 1] * len(widths) / half
+        todo(piece + depth - 1, 0.3 + 0.3 * share, solve, piece)
         for j in range(spans):
-            todo(piece + 1, 0.5, product, piece, j)
-        todo(piece + 1, 0.3, finish, piece)
-        todo(piece + 1, 0.0, give, piece)
+            todo(piece + depth - 1, 0.2 + 0.3 * share, product, piece, j)
+        todo(piece + depth - 1, 0.3 * share, finish, piece)
+        todo(piece + depth - 1, 0.0, give, piece)
 
     pl.semaphore_wait(barrier, 3 + 2 * below.astype(jnp.int32) + 2 * above.astype(jnp.int32))
     send_own(0)
@@ -410,34 +415,49 @@
     pick(1)
     pick(2)
     send_own(1)
-    slots = depth
-
-    for piece in range(pieces):
-        if 0 < piece and piece + 1 < pieces:
-            send_own(piece + 1)
-        left = sum(w for e, w, _ in work if e <= pieces - 1)
-        quota = left / (pieces - piece) / slots
+    send_own(2)
+    steps = pieces + depth - 2
+    marks, released = [], [0]
+
+    def release(end):
+        for when, copy in started[released[0]:end]:
+            if when is None:
+                copy.wait_send()
+            else:
+                pl.when(when)(copy.wait_send)
+        released[0] = max(end, released[0])
+
+
+    for step in range(steps):
+        if 0 < step and step + 2 < pieces:
+            send_own(step + 2)
+        left = sum(w for e, w, _ in work if e < steps)
+        quota = left / (steps - step) / depth
 
         def run():
             spent = 0.0
-            while work and work[0][0] <= piece and (spent < quota or work[0][1] == 0.0):
+            while work and work[0][0] <= step and (spent < quota or work[0][1] == 0.0):
                 spent += work[0][1]
                 work.pop(0)[2]()
 
-        relay_cross(piece)
-        run()
+        if step < pieces:
+            relay_cross(step)
         for d in range(1, depth):
-            relay(piece, d)
+            if 0 <= step + 1 - d < pieces:
+                relay(step + 1 - d, d)
+        for _ in range(depth):
             run()
-    for _, _, call in work:
+        marks.append(len(started))
+        if step >= 3:
+            release(marks[step - 3])
+    for count, (_, _, call) in enumerate(work):
         call()
-    for piece in range(1, pieces):
+        if count == 0:
+            release(marks[-3])
+    for piece in range(1, pieces - 1):
         receive(piece)
-    for when, copy in started:
-        if when is None:
-            copy.wait_send()
-        else:
-            pl.when(when)(copy.wait_send)
+    release(len(started))
+    receive(pieces - 1)
 
 
 def local(n, dosage, covariates, expression, block_index, expr_row):
@@ -446,13 +466,13 @@
     samples, genes = expression.shape
     variants = blocks * block_width
     half = variants // 2
-    width = half // CHUNKS
+    tallest = max(PATTERN) * half // sum(PATTERN)
     scale = math.sqrt(samples - covars - 1)
     vmem = pl.BlockSpec(memory_space=pltpu.VMEM)
     smem = pl.BlockSpec(memory_space=pltpu.SMEM)
     hbm = pl.BlockSpec(memory_space=pl.ANY)
     depth = n // 4
-    pieces = CHUNKS + 1
+    pieces = len(PATTERN) + 1
     sends = pieces * (7 + 2 + 4 * (depth - 1)) + 64
     square = pltpu.VMEM((covars, covars), jnp.float32)
     quarters = 4
@@ -476,8 +496,8 @@
             pltpu.VMEM((8, genes), jnp.float32),
             pltpu.VMEM((half, genes), jnp.float32),
             square, square, square, square,
-            pltpu.VMEM((width, 3 * covars), jnp.bfloat16),
-            pltpu.VMEM((width, 1), jnp.float32),
+            pltpu.VMEM((tallest, 3 * covars), jnp.bfloat16),
+            pltpu.VMEM((tallest, 1), jnp.float32),
             pltpu.VMEM((half, genes), jnp.float32),
             pltpu.SemaphoreType.DMA((quarters,)),
             pltpu.SemaphoreType.DMA,

time: 127 us -> 120 us (0.945)
  Pallas kernels: 122 us -> 115 us
    pallas_call x1, Pallas kernels: 122 us -> 115 us  [local(): pl.pallas_call(functools.partial(exchange, n, scale), out_shape=jax.Shape...]
where the time goes in v2:
time: 120 us; the launch traced here: 119 us
  Pallas kernels  115 us (96%)
  local copies, waits for them, and re-layouts  4.64 us (4%)
    pallas_call x1, Pallas kernels, local(): pl.pallas_call(functools.partial(exchange, n, scale), out_shape=jax.Shape...  115 us
    unnamed x1, local copies, waits for them, and re-layouts  4.64 us

profile of v2, /device:TPU:1, one launch (start us, length us, event | category | flops | bytes accessed | tf_op | source)
XLA Modules:
  0.0 119.3 jit_solution(14479905466414021727)
XLA Ops:
  0.0 114.6 %shard_map.55 = f32[2048,512]{1,0:T(8,128)} custom-call(bf16[256,8192]{1,0:T(8,128)(2,1)} %dosage.1, bf16[96,256]{1,0:T(8,128)(2,1)} %bitcast.1, bf16[4096,512]{1,0:T(8,128)(2,1)} %expr.1, s32[2,1024]{1,0:T(2,128)} %index_ref.1, s32[4096]{0:T(1024)} %row_ref.1), custom_call_target="tpu_custom_call" | custom-call | tf_op jit(solution)/shard_map/pallas_call | solution.py:479
  114.6 4.6 %copy.7 = f32[2048,512]{1,0:T(8,128)} copy(f32[2048,512]{1,0:T(8,128)} %shard_map.55) | data formatting | bytes 8388608
